TPU v7x, 32 devices: a whole 2x2x4 slice. The times are simulated.
32 devices in a mesh: row: 8 (over z, y), col: 4 (over x, core).
Axes of the slice: x: 2, y: 2, z: 4, core: 2. Of those that a mesh axis runs over, the one named last changes fastest.
Arguments:
- eigvec: float32 [32, 8, 128, 1024], P(None, 'row', None, 'col'), may hold values from -6 to 6
- reflectors: float32 [2, 32, 8, 256, 128], P(None, None, 'row', 'col'), may hold values from -6 to 6
- sweep_group: int32 [2, 32, 8], P(None, None, 'row'), may hold values from -1 to 254, as said below
Outputs:
- transformed: float32 [32, 8, 128, 1024], P(None, 'row', None, 'col')
Inputs may be any that keep to these rules, and one draw needn't show every extreme that they name: `sweep_group`: -1 where no diamond sits at that diagonal and tile position (tile position l * R + r for entry [d, l, r]); otherwise the diamond's sweep group, at most its tile position. Within one diagonal no two diamonds sit at adjacent tile positions, and none sits at the last tile position 255.
All inputs are finite; a program needn't handle non-finite values.
Results may differ from a plain program's by a relative error of at most 0.0003.
Values sent between devices are 32-bit elements.
A program may use at most 128 MiB of HBM per device.

v0:
```python
import functools

import jax
import jax.numpy as jnp
from jax import lax
from jax.experimental import pallas as pl
from jax.experimental.pallas import tpu as pltpu
from jax.sharding import PartitionSpec as P


GROUP = 2
CHUNKS = 2
PROFILES = ((11, 9, 9, 11), (12, 10, 10, 12), (13, 11, 11, 13), (14, 12, 12, 14), (16, 14, 14, 16))
GROUPED = 4


def split(x):
    high = x.astype(jnp.bfloat16)
    return high, (x - high.astype(jnp.float32)).astype(jnp.bfloat16)


def dot(a, b):
    return jnp.dot(a, b, preferred_element_type=jnp.float32)


def dot3(a, b):
    return dot(a[1], b[0]) + dot(a[0], b[1]) + dot(a[0], b[0])


def bounds(slots):
    inner = [slots * i // CHUNKS // GROUP * GROUP for i in range(CHUNKS)]
    return inner + [slots]


def chunk_shapes(slots, tiles):
    edges = bounds(slots)
    return [
        jax.ShapeDtypeStruct((high - low,) + tiles.shape[1:], tiles.dtype)
        for low, high in zip(edges[:-1], edges[1:])
    ]


def slot_of(chunks, k):
    for chunk in chunks:
        if k < chunk.shape[0]:
            return chunk.at[k]
        k -= chunk.shape[0]


def gather_kernel(slots, own, behind, panels, tiles, picked, *rest):
    diagonals = panels.shape[0]
    sent, sems = rest[:-1], rest[-1]

    def panel_copy(d, k):
        return pltpu.make_async_copy(
            panels.at[d, own[d, k]], picked.at[d, k], sems.at[d * slots + k]
        )

    def tile_copy(k):
        return pltpu.make_async_copy(
            tiles.at[behind[0, k]], slot_of(sent, k), sems.at[diagonals * slots + k]
        )

    for k in range(slots):
        tile_copy(k).start()
    for d in range(diagonals):
        for k in range(slots):
            panel_copy(d, k).start()
    for k in range(slots):
        tile_copy(k).wait()
    for d in range(diagonals):
        for k in range(slots):
            panel_copy(d, k).wait()


def gather(slots, own, behind, panels, tiles):
    diagonals = panels.shape[0]
    any_spec = pl.BlockSpec(memory_space=pl.ANY)
    return pl.pallas_call(
        functools.partial(gather_kernel, slots),
        grid_spec=pltpu.PrefetchScalarGridSpec(
            num_scalar_prefetch=2,
            grid=(1,),
            in_specs=[any_spec, any_spec],
            out_specs=[pl.BlockSpec(memory_space=pltpu.VMEM)] * (1 + CHUNKS),
            scratch_shapes=[pltpu.SemaphoreType.DMA(((diagonals + 1) * slots,))],
        ),
        out_shape=[
            jax.ShapeDtypeStruct((diagonals, slots) + panels.shape[2:], panels.dtype),
        ] + chunk_shapes(slots, tiles),
        name="gather",
    )(own, behind, panels, tiles)


def scatter_kernel(slots, diagonal, more, behind, counts, tiles, *rest):
    returned, out, sent, sems = rest[:CHUNKS], rest[CHUNKS], rest[CHUNKS + 1:-1], rest[-1]

    def put(k):
        return pltpu.make_async_copy(
            slot_of(returned, k), out.at[behind[diagonal, k]], sems.at[k]
        )

    for k in range(slots):
        @pl.when(k < counts[1, diagonal])
        def _():
            put(k).start()
    for k in range(slots):
        @pl.when(k < counts[1, diagonal])
        def _():
            put(k).wait()
    if more:

        def take(k):
            return pltpu.make_async_copy(
                out.at[behind[diagonal + 1, k]], slot_of(sent, k), sems.at[slots + k]
            )

        for k in range(slots):
            take(k).start()
        for k in range(slots):
            take(k).wait()


def scatter(slots, diagonal, more, behind, counts, tiles, returned):
    any_spec = pl.BlockSpec(memory_space=pl.ANY)
    vmem_spec = pl.BlockSpec(memory_space=pltpu.VMEM)
    shapes = [jax.ShapeDtypeStruct(tiles.shape, tiles.dtype)]
    if more:
        shapes += chunk_shapes(slots, tiles)
    return pl.pallas_call(
        functools.partial(scatter_kernel, slots, diagonal, more),
        grid_spec=pltpu.PrefetchScalarGridSpec(
            num_scalar_prefetch=2,
            grid=(1,),
            in_specs=[any_spec] + [vmem_spec] * CHUNKS,
            out_specs=[any_spec] + [vmem_spec] * (len(shapes) - 1),
            scratch_shapes=[pltpu.SemaphoreType.DMA((2 * slots,))],
        ),
        out_shape=shapes,
        input_output_aliases={2: 0},
        name="scatter",
    )(behind, counts, tiles, *returned)


def factor_kernel(pieces_count, col_ref, *refs):
    pieces = refs[:pieces_count]
    vh_ref, vl_ref, yh_ref, yl_ref = refs[pieces_count:]
    me = col_ref[0]
    group = pieces[0].shape[1]
    band = pieces[0].shape[-1]
    depth = pieces_count * pieces[0].shape[2]
    row = lax.broadcasted_iota(jnp.int32, (depth, band), 0)
    col = lax.broadcasted_iota(jnp.int32, (depth, band), 1)
    inside = (row >= col + 1) & (row <= col + band)
    leading = row == col + 1
    r = lax.broadcasted_iota(jnp.int32, (band, band), 0)
    c = lax.broadcasted_iota(jnp.int32, (band, band), 1)
    slots = range(group)
    vs, ts, factors, inverses = [], [], [], []
    for g in slots:
        parts = [piece[0, g] for piece in pieces]
        stride = 1
        while stride < pieces_count:
            odd = (me // stride) % 2 == 1
            parts = [
                jnp.where(odd, parts[j ^ stride], parts[j]) for j in range(pieces_count)
            ]
            stride *= 2
        panel = jnp.concatenate(parts, axis=0)
        v = jnp.where(leading, 1.0, jnp.where(inside, panel, 0.0))
        vs.append(split(v))
        ts.append(split(v.T))
        vh_ref[g] = vs[g][0]
        vl_ref[g] = vs[g][1]
    for g in slots:
        gram = dot3(ts[g], vs[g])
        diagonal = jnp.sum(jnp.where(r == c, gram, 0.0), axis=0, keepdims=True)
        factors.append(gram)
        inverses.append(jnp.where(r == c, 2.0 / diagonal, 0.0))

    def level(n, inverses):
        coupling = ((r >> n) != (c >> n)) & ((r >> (n + 1)) == (c >> (n + 1))) & (r < c)
        inverse_parts = [split(inverse) for inverse in inverses]
        middles = [
            split(dot3(split(jnp.where(coupling, factors[g], 0.0)), inverse_parts[g]))
            for g in slots
        ]
        return tuple(inverses[g] - dot3(inverse_parts[g], middles[g]) for g in slots)

    inverses = lax.fori_loop(0, (band - 1).bit_length(), level, tuple(inverses))
    for g in slots:
        high, low = split(dot3(split(inverses[g]), ts[g]))
        yh_ref[g] = high
        yl_ref[g] = low


def factor(first, slots, diagonal, col, pieces):
    count = len(pieces)
    _, _, height, band = pieces[0].shape
    depth = count * height
    group = GROUP if slots % GROUP == 0 else 1
    start = first // group
    kind = jnp.bfloat16
    return pl.pallas_call(
        functools.partial(factor_kernel, count),
        grid_spec=pltpu.PrefetchScalarGridSpec(
            num_scalar_prefetch=1,
            grid=(slots // group,),
            in_specs=[
                pl.BlockSpec((1, group, height, band), lambda k, c: (diagonal, k + start, 0, 0))
            ] * count,
            out_specs=[pl.BlockSpec((group, depth, band), lambda k, c: (k, 0, 0))] * 2
            + [pl.BlockSpec((group, band, depth), lambda k, c: (k, 0, 0))] * 2,
        ),
        out_shape=[jax.ShapeDtypeStruct((slots, depth, band), kind)] * 2
        + [jax.ShapeDtypeStruct((slots, band, depth), kind)] * 2,
        name="factor",
    )(col, *pieces)


def apply_kernel(diagonal, first, own, counts, tile, below, vh, vl, yh, yl, tile_out, below_out):
    k = pl.program_id(0) + first
    band = tile.shape[1]
    upper, lower = tile[0], below[0]
    stacked = jnp.concatenate([upper, lower], axis=0)
    solved = dot3((yh[0], yl[0]), split(stacked))
    change = dot3((vh[0], vl[0]), split(solved))
    active = k < counts[0, diagonal]
    tile_out[0] = jnp.where(active, upper - change[:band], upper)
    below_out[0] = jnp.where(active, lower - change[band:], lower)


def apply(first, diagonal, own, counts, tiles, beneath, vh, vl, yh, yl):
    _, band, columns = tiles.shape
    depth = vh.shape[1]
    at_slot = lambda k, own, counts: (k, 0, 0)
    at_own = lambda k, own, counts: (own[diagonal, k + first], 0, 0)
    return pl.pallas_call(
        functools.partial(apply_kernel, diagonal, first),
        grid_spec=pltpu.PrefetchScalarGridSpec(
            num_scalar_prefetch=2,
            grid=(beneath.shape[0],),
            in_specs=[
                pl.BlockSpec((1, band, columns), at_own),
                pl.BlockSpec((1, band, columns), at_slot),
                pl.BlockSpec((1, depth, band), at_slot),
                pl.BlockSpec((1, depth, band), at_slot),
                pl.BlockSpec((1, band, depth), at_slot),
                pl.BlockSpec((1, band, depth), at_slot),
            ],
            out_specs=[
                pl.BlockSpec((1, band, columns), at_own),
                pl.BlockSpec((1, band, columns), at_slot),
            ],
        ),
        out_shape=[
            jax.ShapeDtypeStruct(tiles.shape, tiles.dtype),
            jax.ShapeDtypeStruct(beneath.shape, beneath.dtype),
        ],
        input_output_aliases={2: 0},
        name="apply",
    )(own, counts, tiles, beneath, vh, vl, yh, yl)


def lift(sent, to_above):
    beneath = []
    for chunk in sent:
        beneath.append(lax.ppermute(chunk, "row", to_above))
    return beneath


def steps(slots, own, behind, counts, tiles, panels):
    row_count = lax.axis_size("row")
    col_count = lax.axis_size("col")
    col = lax.axis_index("col").astype(jnp.int32)[None]
    diagonals = panels.shape[0]
    to_above = [(i, (i - 1) % row_count) for i in range(row_count)]
    to_below = [(i, (i + 1) % row_count) for i in range(row_count)]
    picked, *sent = gather(slots, own, behind, panels, tiles)
    beneath = lift(sent, to_above)
    pieces = {0: picked}
    stride = col_count // 2
    while stride >= 1:
        swap = [(i, i ^ stride) for i in range(col_count)]
        pieces.update(
            {q ^ stride: lax.ppermute(p, "col", swap) for q, p in pieces.items()}
        )
        stride //= 2
    pieces = [pieces[q] for q in range(col_count)]
    for diagonal in range(diagonals):
        returned = []
        for first, chunk in zip(bounds(slots), beneath):
            factors = factor(first, chunk.shape[0], diagonal, col, pieces)
            tiles, lower = apply(first, diagonal, own, counts, tiles, chunk, *factors)
            returned.append(lax.ppermute(lower, "row", to_below))
        more = diagonal + 1 < diagonals
        tiles, *sent = scatter(slots, diagonal, more, behind, counts, tiles, returned)
        if more:
            beneath = lift(sent, to_above)
    return tiles


def share_kernel(flags, out, held, send, recv):
    count = held.shape[0]
    me = lax.axis_index("row")
    barrier = pltpu.get_barrier_semaphore()
    mesh_id = pl.DeviceIdType.MESH
    others = [lax.rem(me + by, count) for by in range(1, count)]
    for other in others:
        pl.semaphore_signal(
            barrier, inc=1, device_id={"row": other}, device_id_type=mesh_id
        )
    pl.semaphore_wait(barrier, count - 1)
    copies = [
        pltpu.make_async_remote_copy(
            src_ref=flags,
            dst_ref=held.at[me],
            send_sem=send.at[i],
            recv_sem=recv.at[i],
            device_id={"row": other},
            device_id_type=mesh_id,
        )
        for i, other in enumerate(others)
    ]
    for copy in copies:
        copy.start()
    held[me] = flags[...]
    for copy in copies:
        copy.wait()
    out[...] = held[...]


def share(flags):
    count = lax.axis_size("row")
    diagonals, depth = flags.shape
    rows, lanes = -(-diagonals // 8) * 8, -(-depth // 128) * 128
    padded = jnp.pad(flags, ((0, rows - diagonals), (0, lanes - depth)))
    vmem_spec = pl.BlockSpec(memory_space=pltpu.VMEM)
    shape = (count, rows, lanes)
    gathered = pl.pallas_call(
        share_kernel,
        out_shape=jax.ShapeDtypeStruct(shape, flags.dtype),
        in_specs=[vmem_spec],
        out_specs=vmem_spec,
        scratch_shapes=[
            pltpu.VMEM(shape, flags.dtype),
            pltpu.SemaphoreType.DMA((count - 1,)),
            pltpu.SemaphoreType.DMA((count - 1,)),
        ],
        compiler_params=pltpu.CompilerParams(collective_id=0, has_side_effects=True),
        name="share",
    )(padded)
    return gathered[:, :diagonals, :depth]


def ordering(active):
    depth = active.shape[-1]
    here = jnp.arange(depth, dtype=jnp.int32)
    on = active.astype(jnp.int32)
    earlier = here[None, :] < here[:, None]
    before = jnp.sum(jnp.where(earlier, on[..., None, :], 0), axis=-1)
    total = jnp.sum(on, axis=-1)
    rank = jnp.where(active, before, total[..., None] + here - before)
    order = jnp.sum(
        jnp.where(rank[..., None, :] == here[:, None], here, 0), axis=-1
    ).astype(jnp.int32)
    return order, total.astype(jnp.int32)


def flipped(index, stride):
    return index + stride - 2 * stride * lax.rem(lax.div(index, stride), 2)


def invert_and_store(panels, first, count, vh_ref, vl_ref, yh_ref, yl_ref):
    depth, band = panels.shape[1:]
    row = lax.broadcasted_iota(jnp.int32, (depth, band), 0)
    col = lax.broadcasted_iota(jnp.int32, (depth, band), 1)
    inside = (row >= col + 1) & (row <= col + band)
    leading = row == col + 1
    r = lax.broadcasted_iota(jnp.int32, (band, band), 0)
    c = lax.broadcasted_iota(jnp.int32, (band, band), 1)
    slots = range(count)
    ts, factors, inverses = [], [], []
    for g in slots:
        v = jnp.where(leading, 1.0, jnp.where(inside, panels[first + g], 0.0))
        vs = split(v)
        ts.append(split(v.T))
        vh_ref[first + g] = vs[0]
        vl_ref[first + g] = vs[1]
        gram = dot3(ts[g], vs)
        diagonal = jnp.sum(jnp.where(r == c, gram, 0.0), axis=0, keepdims=True)
        factors.append(gram)
        inverses.append(jnp.where(r == c, 2.0 / diagonal, 0.0))

    def level(n, inverses):
        coupling = ((r >> n) != (c >> n)) & ((r >> (n + 1)) == (c >> (n + 1))) & (r < c)
        inverse_parts = [split(inverse) for inverse in inverses]
        middles = [
            split(dot3(split(jnp.where(coupling, factors[g], 0.0)), inverse_parts[g]))
            for g in slots
        ]
        return tuple(inverses[g] - dot3(inverse_parts[g], middles[g]) for g in slots)

    inverses = lax.fori_loop(0, (band - 1).bit_length(), level, tuple(inverses))
    for g in slots:
        high, low = split(dot3(split(inverses[g]), ts[g]))
        yh_ref[first + g] = high
        yl_ref[first + g] = low


def whole_kernel(
    profile, group, table, tiles_in, panels_in, out,
    tiles, pieces, panel, vh, vl, yh, yl, lift_out, lift_in, upper_new, lower_new, back_in,
    merged, in_sems, panel_sems, lift_sems, back_sems, out_sems,
):
    n0, b0, b1, n1 = profile
    slots, lifts, backs = (n0, n1), (n0, b1), (b0, n1)
    depth = tiles.shape[0]
    height = pieces.shape[2]
    rows = lax.axis_size("row")
    cols = lax.axis_size("col")
    me_row = lax.axis_index("row")
    me_col = lax.axis_index("col")
    above = lax.rem(me_row + rows - 1, rows)
    below = lax.rem(me_row + 1, rows)
    mesh_id = pl.DeviceIdType.MESH
    strides = []
    stride = cols // 2
    while stride >= 1:
        strides.append(stride)
        stride //= 2
    own = lambda d, k: table[d, k]
    behind = lambda d, k: table[2 + d, k]
    upper_slot = lambda d, j: table[4 + d, j]
    lower_slot = lambda d, j: table[6 + d, j]

    panels_copy = pltpu.make_async_copy(panels_in, pieces, in_sems.at[0])
    tiles_copy = pltpu.make_async_copy(tiles_in, tiles, in_sems.at[1])
    panels_copy.start()
    tiles_copy.start()

    barrier = pltpu.get_barrier_semaphore()
    peers = [{"row": above}, {"row": below}]
    peers += [{"col": flipped(me_col, s)} for s in strides]
    for peer in peers:
        pl.semaphore_signal(barrier, inc=1, device_id=peer, device_id_type=mesh_id)
    pl.semaphore_wait(barrier, len(peers))

    def exchange(d, g, stage):
        held = [me_col]
        for s in strides[:stage]:
            held += [flipped(h, s) for h in held]
        base = sum(2**i for i in range(stage))
        copies = []
        for i, h in enumerate(held):
            where = (pl.ds(g * group, group), pl.ds(pl.multiple_of(h * height, height), height))
            copies.append(
                pltpu.make_async_remote_copy(
                    src_ref=panel[d].at[where],
                    dst_ref=panel[d].at[where],
                    send_sem=panel_sems[d].at[0, g, base + i],
                    recv_sem=panel_sems[d].at[1, g, base + i],
                    device_id={"col": flipped(me_col, strides[stage])},
                    device_id_type=mesh_id,
                )
            )
        return copies

    def lift(d, k):
        return pltpu.make_async_remote_copy(
            src_ref=lift_out[d].at[k],
            dst_ref=lift_in[d].at[k],
            send_sem=lift_sems[d].at[0, k],
            recv_sem=lift_sems[d].at[1, k],
            device_id={"row": above},
            device_id_type=mesh_id,
        )

    def give_back(d, k):
        return pltpu.make_async_remote_copy(
            src_ref=lower_new[d].at[k],
            dst_ref=back_in[d].at[k],
            send_sem=back_sems[d].at[0, k],
            recv_sem=back_sems[d].at[1, k],
            device_id={"row": below},
            device_id_type=mesh_id,
        )

    def pick_panels(d):
        mine = pl.ds(pl.multiple_of(me_col * height, height), height)

        def one(g, _):
            for i in range(group):
                panel[d][g * group + i, mine] = pieces[d, own(d, g * group + i)]
            if strides:
                for copy in exchange(d, g, 0):
                    copy.start()
            return 0

        lax.fori_loop(0, panel[d].shape[0] // group, one, 0)

    def forward(d, g):
        for stage in range(1, len(strides)):
            for copy in exchange(d, g, stage - 1):
                copy.wait_recv()
            for copy in exchange(d, g, stage):
                copy.start()

    def factor(d):
        count = panel[d].shape[0] // group

        def one(g, _):
            if strides:
                for copy in exchange(d, g, len(strides) - 1):
                    copy.wait_recv()

            @pl.when(g + 1 < count)
            def _():
                forward(d, g + 1)

            invert_and_store(panel[d], g * group, group, vh[d], vl[d], yh[d], yl[d])
            return 0

        forward(d, 0)
        lax.fori_loop(0, count, one, 0)

    def after_first(j):
        u, l = upper_slot(0, j), lower_slot(0, j)
        kept = jnp.where(l >= 0, back_in[0][jnp.maximum(l, 0)], tiles[j])
        return jnp.where(u >= 0, upper_new[0][jnp.maximum(u, 0)], kept)

    def send_lifts(d, value):
        def one(k, _):
            lift_out[d][k] = value(behind(d, k))

            @pl.when(k > 0)
            def _():
                lift(d, k - 1).start()

            return 0

        lax.fori_loop(0, lifts[d], one, 0)
        lift(d, lifts[d] - 1).start()

    def reflect(d, upper_of, lower_of):
        def one(k, _):
            @pl.when(k < lifts[d])
            def _():
                lift(d, k).wait_recv()

            upper, lower = upper_of(k), lower_of(k)
            band = upper.shape[0]
            stacked = split(jnp.concatenate([upper, lower], axis=0))
            solved = split(dot3((yh[d][k], yl[d][k]), stacked))
            change = dot3((vh[d][k], vl[d][k]), solved)
            lower_new[d][k] = lower - change[band:]
            upper_new[d][k] = upper - change[:band]

            @pl.when(k < backs[d])
            def _():
                give_back(d, k).start()

            return 0

        lax.fori_loop(0, slots[d], one, 0)

    def receive(d):
        def one(k, _):
            give_back(d, k).wait_recv()
            return 0

        lax.fori_loop(0, backs[d], one, 0)

    panels_copy.wait()
    pick_panels(0)
    tiles_copy.wait()
    send_lifts(0, lambda j: tiles[j])
    pick_panels(1)
    factor(0)
    reflect(0, lambda k: tiles[own(0, k)], lambda k: lift_in[0][k])
    factor(1)
    receive(0)
    send_lifts(1, after_first)

    def second_lower(k):
        kept = upper_slot(0, own(1, k))
        return jnp.where(kept >= 0, lower_new[0][jnp.maximum(kept, 0)], lift_in[1][k])

    reflect(1, lambda k: after_first(own(1, k)), second_lower)

    def merge(j, _):
        u = upper_slot(1, j)
        merged[j] = jnp.where(u >= 0, upper_new[1][jnp.maximum(u, 0)], after_first(j))
        return 0

    lax.fori_loop(0, depth, merge, 0)
    receive(1)

    def write(j):
        return pltpu.make_async_copy(merged.at[j], out.at[j], out_sems.at[j])

    def finish(j, _):
        l = lower_slot(1, j)
        merged[j] = jnp.where(l >= 0, back_in[1][jnp.maximum(l, 0)], merged[j])

        @pl.when(j > 0)
        def _():
            write(j - 1).start()

        return 0

    lax.fori_loop(0, depth, finish, 0)
    write(depth - 1).start()

    def drain(j, _):
        write(j).wait()
        return 0

    for d in range(2):
        for g in range(panel[d].shape[0] // group):
            for stage in range(len(strides)):
                for copy in exchange(d, g, stage):
                    copy.wait_send()

        def sent(k, _):
            lift(d, k).wait_send()
            return 0

        def returned(k, _):
            give_back(d, k).wait_send()
            return 0

        lax.fori_loop(0, lifts[d], sent, 0)
        lax.fori_loop(0, backs[d], returned, 0)
    lax.fori_loop(0, depth, drain, 0)


def whole(profile, index, table, tiles, panels):
    depth, band, columns = tiles.shape
    _, _, height, _ = panels.shape
    cols = lax.axis_size("col")
    long = height * cols
    n0, b0, b1, n1 = profile
    group = GROUPED
    padded = [-(-n // group) * group for n in (n0, n1)]
    f32, bf16 = jnp.float32, jnp.bfloat16
    tile_slots = lambda counts: [pltpu.VMEM((n, band, columns), f32) for n in counts]
    dma = pltpu.SemaphoreType.DMA
    scratch = [
        pltpu.VMEM(tiles.shape, f32),
        pltpu.VMEM(panels.shape, f32),
        [pltpu.VMEM((n, long, band), f32) for n in padded],
        [pltpu.VMEM((n, long, band), bf16) for n in padded],
        [pltpu.VMEM((n, long, band), bf16) for n in padded],
        [pltpu.VMEM((n, band, long), bf16) for n in padded],
        [pltpu.VMEM((n, band, long), bf16) for n in padded],
        tile_slots((n0, b1)),
        tile_slots((n0, n1)),
        tile_slots((n0, n1)),
        tile_slots((n0, n1)),
        tile_slots((b0, n1)),
        pltpu.VMEM(tiles.shape, f32),
        dma((2,)),
        [dma((2, n // group, max(cols - 1, 1))) for n in padded],
        [dma((2, n)) for n in (n0, b1)],
        [dma((2, n)) for n in (b0, n1)],
        dma((depth,)),
    ]
    any_spec = pl.BlockSpec(memory_space=pl.ANY)
    return pl.pallas_call(
        functools.partial(whole_kernel, profile, group),
        in_specs=[pl.BlockSpec(memory_space=pltpu.SMEM), any_spec, any_spec],
        out_specs=any_spec,
        out_shape=jax.ShapeDtypeStruct(tiles.shape, tiles.dtype),
        scratch_shapes=scratch,
        compiler_params=pltpu.CompilerParams(
            collective_id=1 + index, has_side_effects=True, vmem_limit_bytes=58 * 2**20
        ),
    )(table, tiles, panels)


def tables(active, row_index):
    rows, _, depth = active.shape
    both = active[:, 0] & active[:, 1]
    single = active & ~both[:, None]
    counts = jnp.sum(active.astype(jnp.int32), axis=-1)
    singles = jnp.sum(single.astype(jnp.int32), axis=-1)
    most, most_single = jnp.max(counts, axis=0), jnp.max(singles, axis=0)
    pair = jnp.stack([row_index, (row_index + rows - 1) % rows])
    on, alone = active[pair], single[pair]
    again = both[pair]
    here = jnp.arange(depth, dtype=jnp.int32)
    earlier = here[None, :] < here[:, None]
    before = lambda x: jnp.sum((earlier & x[..., None, :]).astype(jnp.int32), axis=-1)
    total = jnp.sum(alone.astype(jnp.int32), axis=-1, keepdims=True)
    rank = jnp.where(alone, before(alone), total + before(again)[:, None])
    slot = jnp.where(on, rank, -1)
    order = jnp.sum(jnp.where(slot[..., None, :] == here[:, None], here, 0), axis=-1)
    first_row = row_index == 0
    behind = jnp.where(first_row, jnp.minimum(order[1] + 1, depth - 1), order[1])
    returned = jnp.where(jnp.stack([alone[1, 0], on[1, 1]]), slot[1], -1)
    shifted = jnp.concatenate([jnp.full((2, 1), -1, slot.dtype), returned[:, :-1]], axis=1)
    returned = jnp.where(first_row, shifted, returned)
    table = jnp.concatenate([order[0], behind, slot[0], returned]).astype(jnp.int32)
    return table, most, most_single


def local(eigvec, reflectors, sweep_group):
    row_index = lax.axis_index("row")
    row_count = lax.axis_size("row")
    depth = eigvec.shape[0]
    diagonals = sweep_group.shape[0]
    active = share(sweep_group[:, :, 0]) >= 0
    tiles, panels = eigvec[:, 0], reflectors[:, :, 0]

    def general(table, active, tiles, panels):
        mine = lax.dynamic_index_in_dim(active, row_index, 0, keepdims=False)
        above = lax.dynamic_index_in_dim(
            active, (row_index + row_count - 1) % row_count, 0, keepdims=False
        )
        order, counts = ordering(jnp.stack([mine, above]))
        own = order[0]
        behind = jnp.where(row_index == 0, (order[1] + 1) % depth, order[1])
        return steps(depth, own, behind, counts, tiles, panels)

    if diagonals != 2:
        return general(None, active, tiles, panels)[:, None]
    table, most, alone = tables(active, row_index)
    profiles = [p for p in PROFILES if max(p) <= depth]
    small = depth <= max(PROFILES[-1])
    if small and (depth,) * 4 not in profiles:
        profiles.append((depth,) * 4)
    needs = (most[0], alone[0], alone[1], most[1])
    choice, missed = jnp.int32(0), jnp.bool_(True)
    for profile in profiles[: len(profiles) - small]:
        fits = functools.reduce(jnp.logical_and, [n <= s for n, s in zip(needs, profile)])
        missed = missed & ~fits
        choice = choice + missed.astype(jnp.int32)

    def branch(index, profile):
        return lambda table, active, tiles, panels: whole(profile, index, table, tiles, panels)

    branches = [branch(i, p) for i, p in enumerate(profiles)]
    if not small:
        branches.append(general)
    args = (table, active, tiles, panels)
    out = lax.switch(choice, branches, *args) if len(branches) > 1 else branches[0](*args)
    return out[:, None]


def solution(mesh):
    return jax.shard_map(
        local,
        mesh=mesh,
        in_specs=(
            P(None, "row", None, "col"),
            P(None, None, "row", "col", None),
            P(None, None, "row"),
        ),
        out_specs=P(None, "row", None, "col"),
        check_vma=False,
    )
```

profile of v0, /device:TPU:0, one launch (start us, length us, event | category | flops | bytes accessed | tf_op | source)
XLA Modules:
  0.0 199.1 jit_solution(13669346342182987553)
XLA Ops:
  0.0 1.3 pad.5.flags
  1.3 9.8 %share.1 = s32[8,8,128]{2,1,0:T(8,128)} custom-call(s32[8,128]{1,0:T(8,128)} %pad.5.flags), custom_call_target="tpu_custom_call" | custom-call | tf_op jit(solution)/shard_map/share/pallas_call | solution.py:340
  11.1 1.0 convert_reduce_fusion.4
  12.1 0.6 fusion.5
  13.4 0.2 convert_reduce_fusion.3
  13.6 0.6 fusion.6
  26.6 0.1 fusion.3
  26.7 0.6 gather_fusion
  27.3 0.6 gather_fusion.1
  27.8 0.2 convert_reduce_fusion.1
  28.0 0.6 gather_fusion.2
  28.6 0.1 convert_reduce_fusion.2
  28.7 0.1 convert_reduce_fusion.5
  28.8 0.1 select_select_fusion
  28.9 0.1 pad_select_fusion
  29.0 0.1 select_reduce_fusion.2
  29.2 0.0 copy-start
  29.2 4.7 %copy.57 = f32[32,128,256]{2,1,0:T(8,128)} copy(f32[32,128,256]{2,1,0:T(8,128)} %bitcast.56) | data formatting | bytes 8388608
  33.9 0.0 copy-done
  33.9 160.5 %conditional.1 = (f32[32,1,128,256]{3,2,1,0:T(8,128)}) conditional(s32[]{:T(128)} %bitcast.22, (s32[8,32]{1,0:T(8,128)S(1)}, f32[32,128,256]{2,1,0:T(8,128)S(1)}, f32[2,32,64,128]{3,2,1,0:T(8,128)}) %tuple.63, (s32[8,32]{1,0:T(8,128)S(1)}, f32[32,128,256]{2,1,0:T(8,128)S(1)}, f32[2,32,64,128]{3,2,1,0:T(8,128)}) %tuple.64, ...), branch_computations={%region_8.9_spmd, %region_9.10_spmd, %region_10.11_spmd, %region_1... | conditional | flops 23249 | bytes 125837328 | solution.py:747
  33.9 160.3 %branch_2_fun.1 = f32[32,128,256]{2,1,0:T(8,128)} custom-call(s32[8,32]{1,0:T(8,128)S(1)} %get-tuple-element.57.table, f32[32,128,256]{2,1,0:T(8,128)S(1)} %get-tuple-element.58.tiles_in, f32[2,32,64,128]{3,2,1,0:T(8,128)} %get-tuple-element.59.panels_in), custom_call_target="tpu_custom_call" | custom-call | tf_op jit(solution)/shard_map/cond/branch_2_fun/pallas_call | solution.py:670
  194.4 4.7 %copy.59 = f32[32,1,128,256]{3,2,1,0:T(8,128)} copy(f32[32,1,128,256]{3,2,1,0:T(8,128)} %get-tuple-element.101) | data formatting | bytes 8388608
  (13 shorter events, 0.1 us)
Async XLA Ops:
  29.2 4.7 %copy-start = (f32[32,1,128,256]{3,2,1,0:T(8,128)S(1)}, f32[32,1,128,256]{3,2,1,0:T(8,128)}, u32[]{:S(2)}) copy-start(f32[32,1,128,256]{3,2,1,0:T(8,128)} %param.9) | copy-start | bytes 12582916
where the time goes:
time: 201 us; the launch traced here: 199 us
  Pallas kernels  170 us (85%)
  local copies, waits for them, and re-layouts  13.6 us (7%)
  between operations  13.1 us (7%)
  other arithmetic  2.08 us (1%)
    pallas_call x1, Pallas kernels, whole(): pl.pallas_call(functools.partial(whole_kernel, profile, group), in_specs=...  160 us
    pallas_call x1, Pallas kernels, share(): pl.pallas_call(share_kernel, out_shape=jax.ShapeDtypeStruct(shape, flags....  9.78 us
    unnamed x5, local copies, waits for them, and re-layouts  9.4 us

commit v1 on v0

--- a/solution.py
+++ b/solution.py
@@ -10,7 +10,10 @@
 
 GROUP = 2
 CHUNKS = 2
-PROFILES = ((11, 9, 9, 11), (12, 10, 10, 12), (13, 11, 11, 13), (14, 12, 12, 14), (16, 14, 14, 16))
+PROFILES = (
+    (12, 4, 4, 12), (12, 5, 5, 12), (13, 5, 5, 13), (13, 5, 6, 14),
+    (15, 6, 6, 15), (16, 7, 7, 16), (20, 12, 12, 20),
+)
 GROUPED = 4
 
 
@@ -300,9 +303,12 @@
     return tiles
 
 
-def share_kernel(flags, out, held, send, recv):
-    count = held.shape[0]
+def plan_kernel(profiles, flags, table, choice, everyone, mine, held, send, recv):
+    count, _, lanes = held.shape
+    diagonals, depth = flags.shape
     me = lax.axis_index("row")
+    mine[...] = jnp.full(mine.shape, -1, mine.dtype)
+    mine[0:diagonals, 0:depth] = flags[...]
     barrier = pltpu.get_barrier_semaphore()
     mesh_id = pl.DeviceIdType.MESH
     others = [lax.rem(me + by, count) for by in range(1, count)]
@@ -313,7 +319,7 @@
     pl.semaphore_wait(barrier, count - 1)
     copies = [
         pltpu.make_async_remote_copy(
-            src_ref=flags,
+            src_ref=mine,
             dst_ref=held.at[me],
             send_sem=send.at[i],
             recv_sem=recv.at[i],
@@ -324,33 +330,183 @@
     ]
     for copy in copies:
         copy.start()
-    held[me] = flags[...]
+    held[me] = mine[...]
     for copy in copies:
         copy.wait()
-    out[...] = held[...]
-
-
-def share(flags):
+    everyone[...] = held[...]
+
+    f32 = jnp.float32
+    row = lax.broadcasted_iota(jnp.int32, (count, lanes), 0)
+    on = [jnp.where(held[:, d, :] >= 0, 1.0, 0.0) for d in range(2)]
+    after = []
+    for x in on:
+        under = pltpu.roll(x, count - 1, axis=0)
+        after.append(jnp.where(row == count - 1, pltpu.roll(under, lanes - 1, axis=1), under))
+    again = on[0] * on[1]
+    first, second = on[0] - again, on[1] - again
+    kinds = [
+        first * after[1],
+        first - first * after[1],
+        again,
+        second - second * after[0],
+        second * after[0],
+    ]
+    sums = [jnp.sum(x, axis=1, keepdims=True) for x in kinds]
+    must, may, rep, ready, unready = sums
+    chosen = [jnp.zeros((1, 1), f32) for _ in range(4)]
+    index, missed = jnp.zeros((1, 1), f32), jnp.ones((1, 1), f32)
+    for early, soon, late, last in profiles:
+        bad = (must + may + rep > early) | (must > soon)
+        bad |= rep + ready + unready + jnp.maximum(must + may - soon, 0.0) > last
+        bad |= unready + jnp.maximum(ready - (early - must - may - rep), 0.0) > late
+        still = missed * jnp.max(jnp.where(bad, 1.0, 0.0), axis=0, keepdims=True)
+        for i, size in enumerate((early, soon, late, last)):
+            chosen[i] = chosen[i] + (missed - still) * size
+        index, missed = index + still, still
+    choice[0] = index[0, 0].astype(jnp.int32)
+    early, soon, late, last = chosen
+
+    above = lax.rem(me + count - 1, count)
+    picked = [
+        jnp.sum(jnp.where(row == who, x, 0.0), axis=0, keepdims=True)
+        for who in (me, above)
+        for x in kinds
+    ]
+    none = jnp.zeros((1, lanes), f32)
+    stacked = jnp.concatenate(picked + [none] * 6, axis=0)
+    r = lax.broadcasted_iota(jnp.int32, (lanes, lanes), 0)
+    c = lax.broadcasted_iota(jnp.int32, (lanes, lanes), 1)
+    ahead = jnp.dot(
+        stacked.astype(jnp.bfloat16),
+        jnp.where(r < c, 1.0, 0.0).astype(jnp.bfloat16),
+        preferred_element_type=f32,
+    )
+    totals = jnp.sum(stacked, axis=1, keepdims=True)
+
+    def places(which):
+        at = [stacked[5 * which + i : 5 * which + i + 1] > 0.5 for i in range(5)]
+        rank = [ahead[5 * which + i : 5 * which + i + 1] for i in range(5)]
+        must, may, rep, ready, unready = [
+            totals[5 * which + i : 5 * which + i + 1] for i in range(5)
+        ]
+        slot0 = jnp.where(
+            at[0],
+            rank[0],
+            jnp.where(at[1], must + rank[1], jnp.where(at[2], must + may + rank[2], -1.0)),
+        )
+        taken = must + may + rep
+        spare = early - taken
+        over = jnp.maximum(ready - spare, 0.0)
+        tardy = over + unready
+        prompt = rep + ready - over
+
+        def placed(p):
+            return jnp.where(p < last - late, p, p + tardy)
+
+        fast = at[3] & (rank[3] < spare)
+        lag = jnp.where(
+            at[4], over + rank[4], jnp.where(at[3] & ~fast, rank[3] - spare, -1.0)
+        )
+        slot1 = jnp.where(
+            at[2],
+            placed(rank[2]),
+            jnp.where(fast, placed(rep + rank[3]), jnp.where(lag >= 0, last - late + lag, -1.0)),
+        )
+        single = at[0] | at[1]
+        held_back = single & (slot0 >= soon)
+        kept = jnp.where(held_back, placed(prompt + slot0 - soon), -1.0)
+        sooner = jnp.where(single & (slot0 < soon), slot0, -1.0)
+        ahead_of = jnp.where(fast, taken + rank[3], -1.0)
+        return at, slot0, slot1, kept, sooner, ahead_of, lag
+
+    at, slot0, slot1, kept, _, ahead_of, _ = places(0)
+    _, up0, up1, up_kept, up_sooner, up_ahead, up_lag = places(1)
+    keys = [
+        slot0,
+        slot1,
+        kept,
+        jnp.maximum(up0, up_ahead),
+        up_lag,
+        jnp.where(at[2], slot0, -1.0),
+        ahead_of,
+        none,
+    ]
+    filler = jnp.zeros((lanes - len(keys), lanes), f32)
+    turned = jnp.concatenate(keys + [filler], axis=0).T
+    column = lambda i: turned[:, i : i + 1]
+    tile = r.astype(f32)
+    place = c.astype(f32)
+
+    def turn(key, value, missing):
+        hit = jnp.where(column(key) == place, value - missing, 0.0)
+        return jnp.sum(hit, axis=0, keepdims=True) + missing
+
+    top = me == 0
+
+    def behind(key):
+        found = turn(key, tile, 0.0)
+        return jnp.where(top, jnp.minimum(found + 1.0, depth - 1.0), found)
+
+    def below(x):
+        return jnp.where(top, pltpu.roll(x, 1, axis=1), x)
+
+    rows = [
+        turn(0, tile, 0.0),
+        turn(1, tile, 0.0),
+        behind(3),
+        behind(4),
+        slot0,
+        slot1,
+        below(up_sooner),
+        below(jnp.maximum(up1, up_kept)),
+        turn(1, column(5), -1.0),
+        turn(1, column(6), -1.0),
+        turn(2, column(0), -1.0),
+    ]
+    rows += [none] * (table.shape[0] - len(rows))
+    table[...] = jnp.concatenate(rows, axis=0).astype(jnp.int32)
+
+
+def plan(profiles, flags):
     count = lax.axis_size("row")
-    diagonals, depth = flags.shape
-    rows, lanes = -(-diagonals // 8) * 8, -(-depth // 128) * 128
-    padded = jnp.pad(flags, ((0, rows - diagonals), (0, lanes - depth)))
+    lanes = 128
     vmem_spec = pl.BlockSpec(memory_space=pltpu.VMEM)
-    shape = (count, rows, lanes)
-    gathered = pl.pallas_call(
-        share_kernel,
-        out_shape=jax.ShapeDtypeStruct(shape, flags.dtype),
+    shape = (count, 8, lanes)
+    kind = flags.dtype
+    return pl.pallas_call(
+        functools.partial(plan_kernel, profiles),
+        out_shape=[
+            jax.ShapeDtypeStruct((16, lanes), kind),
+            jax.ShapeDtypeStruct((1,), kind),
+            jax.ShapeDtypeStruct(shape, kind),
+        ],
         in_specs=[vmem_spec],
-        out_specs=vmem_spec,
+        out_specs=[vmem_spec, pl.BlockSpec(memory_space=pltpu.SMEM), vmem_spec],
         scratch_shapes=[
-            pltpu.VMEM(shape, flags.dtype),
+            pltpu.VMEM(shape[1:], kind),
+            pltpu.VMEM(shape, kind),
             pltpu.SemaphoreType.DMA((count - 1,)),
             pltpu.SemaphoreType.DMA((count - 1,)),
         ],
         compiler_params=pltpu.CompilerParams(collective_id=0, has_side_effects=True),
-        name="share",
-    )(padded)
-    return gathered[:, :diagonals, :depth]
+        name="plan",
+    )(flags)
+
+
+def fresh_kernel(x, out):
+    out[...] = x[...]
+
+
+def fresh(x):
+    spec = pl.BlockSpec((1,) + x.shape[1:], lambda k: (k, 0, 0))
+    return pl.pallas_call(
+        fresh_kernel,
+        grid=(x.shape[0],),
+        in_specs=[spec],
+        out_specs=spec,
+        out_shape=jax.ShapeDtypeStruct(x.shape, x.dtype),
+        name="fresh",
+    )(x)
 
 
 def ordering(active):
@@ -413,8 +569,9 @@
     tiles, pieces, panel, vh, vl, yh, yl, lift_out, lift_in, upper_new, lower_new, back_in,
     merged, in_sems, panel_sems, lift_sems, back_sems, out_sems,
 ):
-    n0, b0, b1, n1 = profile
-    slots, lifts, backs = (n0, n1), (n0, b1), (b0, n1)
+    early, soon, late, last = profile
+    slots, lifts, backs = (early, last), (early, late), (soon, last)
+    skip = (0, last - late)
     depth = tiles.shape[0]
     height = pieces.shape[2]
     rows = lax.axis_size("row")
@@ -433,6 +590,10 @@
     behind = lambda d, k: table[2 + d, k]
     upper_slot = lambda d, j: table[4 + d, j]
     lower_slot = lambda d, j: table[6 + d, j]
+
+    def either(source, index, other):
+        return jnp.where(index >= 0, source[jnp.maximum(index, 0)], other)
+
 
     panels_copy = pltpu.make_async_copy(panels_in, pieces, in_sems.at[0])
     tiles_copy = pltpu.make_async_copy(tiles_in, tiles, in_sems.at[1])
@@ -469,7 +630,7 @@
     def lift(d, k):
         return pltpu.make_async_remote_copy(
             src_ref=lift_out[d].at[k],
-            dst_ref=lift_in[d].at[k],
+            dst_ref=lift_in[d].at[skip[d] + k],
             send_sem=lift_sems[d].at[0, k],
             recv_sem=lift_sems[d].at[1, k],
             device_id={"row": above},
@@ -525,9 +686,8 @@
         lax.fori_loop(0, count, one, 0)
 
     def after_first(j):
-        u, l = upper_slot(0, j), lower_slot(0, j)
-        kept = jnp.where(l >= 0, back_in[0][jnp.maximum(l, 0)], tiles[j])
-        return jnp.where(u >= 0, upper_new[0][jnp.maximum(u, 0)], kept)
+        kept = either(back_in[0], lower_slot(0, j), tiles[j])
+        return either(upper_new[0], upper_slot(0, j), kept)
 
     def send_lifts(d, value):
         def one(k, _):
@@ -542,18 +702,18 @@
         lax.fori_loop(0, lifts[d], one, 0)
         lift(d, lifts[d] - 1).start()
 
-    def reflect(d, upper_of, lower_of):
+    def reflect(d, upper_of, lower_of, sent_of):
         def one(k, _):
-            @pl.when(k < lifts[d])
+            @pl.when(k >= skip[d])
             def _():
-                lift(d, k).wait_recv()
+                lift(d, k - skip[d]).wait_recv()
 
             upper, lower = upper_of(k), lower_of(k)
             band = upper.shape[0]
             stacked = split(jnp.concatenate([upper, lower], axis=0))
             solved = split(dot3((yh[d][k], yl[d][k]), stacked))
             change = dot3((vh[d][k], vl[d][k]), solved)
-            lower_new[d][k] = lower - change[band:]
+            lower_new[d][k] = sent_of(k, lower - change[band:])
             upper_new[d][k] = upper - change[:band]
 
             @pl.when(k < backs[d])
@@ -577,20 +737,24 @@
     send_lifts(0, lambda j: tiles[j])
     pick_panels(1)
     factor(0)
-    reflect(0, lambda k: tiles[own(0, k)], lambda k: lift_in[0][k])
+    reflect(0, lambda k: tiles[own(0, k)], lambda k: lift_in[0][k], lambda k, lower: lower)
     factor(1)
     receive(0)
     send_lifts(1, after_first)
 
     def second_lower(k):
-        kept = upper_slot(0, own(1, k))
-        return jnp.where(kept >= 0, lower_new[0][jnp.maximum(kept, 0)], lift_in[1][k])
-
-    reflect(1, lambda k: after_first(own(1, k)), second_lower)
+        arrived = either(lift_in[0], table[9, k], lift_in[1][k])
+        return either(lower_new[0], table[8, k], arrived)
+
+    reflect(
+        1,
+        lambda k: after_first(own(1, k)),
+        second_lower,
+        lambda k, lower: either(lower_new[0], table[10, k], lower),
+    )
 
     def merge(j, _):
-        u = upper_slot(1, j)
-        merged[j] = jnp.where(u >= 0, upper_new[1][jnp.maximum(u, 0)], after_first(j))
+        merged[j] = either(upper_new[1], upper_slot(1, j), after_first(j))
         return 0
 
     lax.fori_loop(0, depth, merge, 0)
@@ -600,8 +764,7 @@
         return pltpu.make_async_copy(merged.at[j], out.at[j], out_sems.at[j])
 
     def finish(j, _):
-        l = lower_slot(1, j)
-        merged[j] = jnp.where(l >= 0, back_in[1][jnp.maximum(l, 0)], merged[j])
+        merged[j] = either(back_in[1], lower_slot(1, j), merged[j])
 
         @pl.when(j > 0)
         def _():
@@ -640,9 +803,9 @@
     _, _, height, _ = panels.shape
     cols = lax.axis_size("col")
     long = height * cols
-    n0, b0, b1, n1 = profile
+    early, soon, late, last = profile
     group = GROUPED
-    padded = [-(-n // group) * group for n in (n0, n1)]
+    padded = [-(-n // group) * group for n in (early, last)]
     f32, bf16 = jnp.float32, jnp.bfloat16
     tile_slots = lambda counts: [pltpu.VMEM((n, band, columns), f32) for n in counts]
     dma = pltpu.SemaphoreType.DMA
@@ -654,16 +817,16 @@
         [pltpu.VMEM((n, long, band), bf16) for n in padded],
         [pltpu.VMEM((n, band, long), bf16) for n in padded],
         [pltpu.VMEM((n, band, long), bf16) for n in padded],
-        tile_slots((n0, b1)),
-        tile_slots((n0, n1)),
-        tile_slots((n0, n1)),
-        tile_slots((n0, n1)),
-        tile_slots((b0, n1)),
+        tile_slots((early, late)),
+        tile_slots((early, last)),
+        tile_slots((early, last)),
+        tile_slots((early, last)),
+        tile_slots((soon, last)),
         pltpu.VMEM(tiles.shape, f32),
         dma((2,)),
         [dma((2, n // group, max(cols - 1, 1))) for n in padded],
-        [dma((2, n)) for n in (n0, b1)],
-        [dma((2, n)) for n in (b0, n1)],
+        [dma((2, n)) for n in (early, late)],
+        [dma((2, n)) for n in (soon, last)],
         dma((depth,)),
     ]
     any_spec = pl.BlockSpec(memory_space=pl.ANY)
@@ -679,72 +842,35 @@
     )(table, tiles, panels)
 
 
-def tables(active, row_index):
-    rows, _, depth = active.shape
-    both = active[:, 0] & active[:, 1]
-    single = active & ~both[:, None]
-    counts = jnp.sum(active.astype(jnp.int32), axis=-1)
-    singles = jnp.sum(single.astype(jnp.int32), axis=-1)
-    most, most_single = jnp.max(counts, axis=0), jnp.max(singles, axis=0)
-    pair = jnp.stack([row_index, (row_index + rows - 1) % rows])
-    on, alone = active[pair], single[pair]
-    again = both[pair]
-    here = jnp.arange(depth, dtype=jnp.int32)
-    earlier = here[None, :] < here[:, None]
-    before = lambda x: jnp.sum((earlier & x[..., None, :]).astype(jnp.int32), axis=-1)
-    total = jnp.sum(alone.astype(jnp.int32), axis=-1, keepdims=True)
-    rank = jnp.where(alone, before(alone), total + before(again)[:, None])
-    slot = jnp.where(on, rank, -1)
-    order = jnp.sum(jnp.where(slot[..., None, :] == here[:, None], here, 0), axis=-1)
-    first_row = row_index == 0
-    behind = jnp.where(first_row, jnp.minimum(order[1] + 1, depth - 1), order[1])
-    returned = jnp.where(jnp.stack([alone[1, 0], on[1, 1]]), slot[1], -1)
-    shifted = jnp.concatenate([jnp.full((2, 1), -1, slot.dtype), returned[:, :-1]], axis=1)
-    returned = jnp.where(first_row, shifted, returned)
-    table = jnp.concatenate([order[0], behind, slot[0], returned]).astype(jnp.int32)
-    return table, most, most_single
-
-
 def local(eigvec, reflectors, sweep_group):
     row_index = lax.axis_index("row")
     row_count = lax.axis_size("row")
     depth = eigvec.shape[0]
-    diagonals = sweep_group.shape[0]
-    active = share(sweep_group[:, :, 0]) >= 0
-    tiles, panels = eigvec[:, 0], reflectors[:, :, 0]
-
-    def general(table, active, tiles, panels):
-        mine = lax.dynamic_index_in_dim(active, row_index, 0, keepdims=False)
-        above = lax.dynamic_index_in_dim(
-            active, (row_index + row_count - 1) % row_count, 0, keepdims=False
-        )
-        order, counts = ordering(jnp.stack([mine, above]))
-        own = order[0]
-        behind = jnp.where(row_index == 0, (order[1] + 1) % depth, order[1])
-        return steps(depth, own, behind, counts, tiles, panels)
-
-    if diagonals != 2:
-        return general(None, active, tiles, panels)[:, None]
-    table, most, alone = tables(active, row_index)
     profiles = [p for p in PROFILES if max(p) <= depth]
     small = depth <= max(PROFILES[-1])
     if small and (depth,) * 4 not in profiles:
         profiles.append((depth,) * 4)
-    needs = (most[0], alone[0], alone[1], most[1])
-    choice, missed = jnp.int32(0), jnp.bool_(True)
-    for profile in profiles[: len(profiles) - small]:
-        fits = functools.reduce(jnp.logical_and, [n <= s for n, s in zip(needs, profile)])
-        missed = missed & ~fits
-        choice = choice + missed.astype(jnp.int32)
+    table, choice, flags = plan(profiles, sweep_group[:, :, 0])
+
+    def general(table, flags, tiles, panels):
+        active = flags[:, : sweep_group.shape[0], :depth] >= 0
+        mine = lax.dynamic_index_in_dim(active, row_index, 0, keepdims=False)
+        above = lax.dynamic_index_in_dim(
+            active, (row_index + row_count - 1) % row_count, 0, keepdims=False
+        )
+        order, counts = ordering(jnp.stack([mine, above]))
+        own = order[0]
+        behind = jnp.where(row_index == 0, (order[1] + 1) % depth, order[1])
+        return steps(depth, own, behind, counts, fresh(tiles), panels)
 
     def branch(index, profile):
-        return lambda table, active, tiles, panels: whole(profile, index, table, tiles, panels)
+        return lambda table, flags, tiles, panels: whole(profile, index, table, tiles, panels)
 
     branches = [branch(i, p) for i, p in enumerate(profiles)]
     if not small:
         branches.append(general)
-    args = (table, active, tiles, panels)
-    out = lax.switch(choice, branches, *args) if len(branches) > 1 else branches[0](*args)
+    args = (table, flags, eigvec[:, 0], reflectors[:, :, 0])
+    out = lax.switch(choice[0], branches, *args) if len(branches) > 1 else branches[0](*args)
     return out[:, None]
 
 

time: 201 us -> 162 us (0.81)
  Pallas kernels: 170 us -> 154 us
  between operations: 13.1 us -> 0.66 us
  local copies, waits for them, and re-layouts: 13.6 us -> 4.66 us
  other arithmetic: 2.08 us -> 0 us
    pallas_call x1, Pallas kernels: 160 us -> 144 us  [whole(): pl.pallas_call(functools.partial(whole_kernel, profile, group), in_specs=...]
    unnamed x5 -> x1, local copies, waits for them, and re-layouts: 9.4 us -> 4.66 us
where the time goes in v1:
time: 162 us; the launch traced here: 160 us
  Pallas kernels  154 us (95%)
  local copies, waits for them, and re-layouts  4.66 us (3%)
    pallas_call x1, Pallas kernels, whole(): pl.pallas_call(functools.partial(whole_kernel, profile, group), in_specs=...  144 us
    pallas_call x1, Pallas kernels, plan(): pl.pallas_call(functools.partial(plan_kernel, profiles), out_shape=[jax.S...  9.91 us
    unnamed x1, local copies, waits for them, and re-layouts  4.66 us

profile of v1, /device:TPU:0, one launch (start us, length us, event | category | flops | bytes accessed | tf_op | source)
XLA Modules:
  0.0 160.0 jit_solution(17198418125039763806)
XLA Ops:
  0.0 9.9 %plan.1 = (s32[16,128]{1,0:T(8,128)S(1)}, s32[1]{0:T(128)}, s32[8,8,128]{2,1,0:T(8,128)S(1)}) custom-call(s32[2,32]{1,0:T(2,128)} %bitcast.51), custom_call_target="tpu_custom_call" | custom-call | tf_op jit(solution)/shard_map/plan/pallas_call | solution.py:476
  10.6 144.7 %conditional.1 = (f32[32,1,128,256]{3,2,1,0:T(8,128)}) conditional(s32[]{:T(128)} %bitcast.28, (s32[16,128]{1,0:T(8,128)S(1)}, f32[32,128,256]{2,1,0:T(8,128)}, f32[2,32,64,128]{3,2,1,0:T(8,128)}) %tuple.72, (s32[16,128]{1,0:T(8,128)S(1)}, f32[32,128,256]{2,1,0:T(8,128)}, f32[2,32,64,128]{3,2,1,0:T(8,128)}) %tuple.73, ...), branch_computations={%region_0.0_spmd, %region_1.0_spmd, %region_2.0_spmd, %region_3.0_... | conditional | flops 23761 | bytes 134228512 | solution.py:873
  10.8 144.2 %branch_4_fun.1 = f32[32,128,256]{2,1,0:T(8,128)} custom-call(s32[16,128]{1,0:T(8,128)S(1)} %get-tuple-element.77.table, f32[32,128,256]{2,1,0:T(8,128)} %get-tuple-element.78.tiles_in, f32[2,32,64,128]{3,2,1,0:T(8,128)} %get-tuple-element.79.panels_in), custom_call_target="tpu_custom_call" | custom-call | tf_op jit(solution)/shard_map/cond/branch_4_fun/pallas_call | solution.py:833
  155.3 4.7 %copy.43 = f32[32,1,128,256]{3,2,1,0:T(8,128)} copy(f32[32,1,128,256]{3,2,1,0:T(8,128)} %get-tuple-element.127) | data formatting | bytes 8388608

commit v2 on v1

--- a/solution.py
+++ b/solution.py
@@ -565,13 +565,14 @@
 
 
 def whole_kernel(
-    profile, group, table, tiles_in, panels_in, out,
-    tiles, pieces, panel, vh, vl, yh, yl, lift_out, lift_in, upper_new, lower_new, back_in,
-    merged, in_sems, panel_sems, lift_sems, back_sems, out_sems,
+    profile, group, table, tiles_in, panels_in, merged, last_back,
+    tiles, pieces, panel, vh, vl, yh, yl, lift_out, lift_in, upper_new, lower_new, first_back,
+    in_sems, panel_sems, lift_sems, back_sems,
 ):
     early, soon, late, last = profile
     slots, lifts, backs = (early, last), (early, late), (soon, last)
     skip = (0, last - late)
+    back_in = (first_back, last_back)
     depth = tiles.shape[0]
     height = pieces.shape[2]
     rows = lax.axis_size("row")
@@ -738,9 +739,9 @@
     pick_panels(1)
     factor(0)
     reflect(0, lambda k: tiles[own(0, k)], lambda k: lift_in[0][k], lambda k, lower: lower)
+    send_lifts(1, lambda j: either(upper_new[0], upper_slot(0, j), tiles[j]))
     factor(1)
     receive(0)
-    send_lifts(1, after_first)
 
     def second_lower(k):
         arrived = either(lift_in[0], table[9, k], lift_in[1][k])
@@ -759,26 +760,6 @@
 
     lax.fori_loop(0, depth, merge, 0)
     receive(1)
-
-    def write(j):
-        return pltpu.make_async_copy(merged.at[j], out.at[j], out_sems.at[j])
-
-    def finish(j, _):
-        merged[j] = either(back_in[1], lower_slot(1, j), merged[j])
-
-        @pl.when(j > 0)
-        def _():
-            write(j - 1).start()
-
-        return 0
-
-    lax.fori_loop(0, depth, finish, 0)
-    write(depth - 1).start()
-
-    def drain(j, _):
-        write(j).wait()
-        return 0
-
     for d in range(2):
         for g in range(panel[d].shape[0] // group):
             for stage in range(len(strides)):
@@ -795,7 +776,43 @@
 
         lax.fori_loop(0, lifts[d], sent, 0)
         lax.fori_loop(0, backs[d], returned, 0)
+
+
+def settle_kernel(table, merged, back, out, sems):
+    depth = merged.shape[0]
+
+    def one(j, _):
+        slot = table[7, j]
+
+        @pl.when(slot >= 0)
+        def _():
+            pltpu.make_async_copy(back.at[jnp.maximum(slot, 0)], out.at[j], sems.at[j]).start()
+
+        @pl.when(slot < 0)
+        def _():
+            pltpu.make_async_copy(merged.at[j], out.at[j], sems.at[j]).start()
+
+        return 0
+
+    def drain(j, _):
+        pltpu.make_async_copy(merged.at[j], out.at[j], sems.at[j]).wait()
+        return 0
+
+    lax.fori_loop(0, depth, one, 0)
     lax.fori_loop(0, depth, drain, 0)
+
+
+def settle(table, merged, back):
+    vmem_spec = pl.BlockSpec(memory_space=pltpu.VMEM)
+    return pl.pallas_call(
+        settle_kernel,
+        in_specs=[pl.BlockSpec(memory_space=pltpu.SMEM), vmem_spec, vmem_spec],
+        out_specs=pl.BlockSpec(memory_space=pl.ANY),
+        out_shape=jax.ShapeDtypeStruct(merged.shape, merged.dtype),
+        scratch_shapes=[pltpu.SemaphoreType.DMA((merged.shape[0],))],
+        compiler_params=pltpu.CompilerParams(vmem_limit_bytes=8 * 2**20),
+        name="settle",
+    )(table, merged, back)
 
 
 def whole(profile, index, table, tiles, panels):
@@ -821,25 +838,32 @@
         tile_slots((early, last)),
         tile_slots((early, last)),
         tile_slots((early, last)),
-        tile_slots((soon, last)),
-        pltpu.VMEM(tiles.shape, f32),
+        pltpu.VMEM((soon, band, columns), f32),
         dma((2,)),
         [dma((2, n // group, max(cols - 1, 1))) for n in padded],
         [dma((2, n)) for n in (early, late)],
         [dma((2, n)) for n in (soon, last)],
-        dma((depth,)),
     ]
+    tile_bytes = band * columns * 4
+    held = 2 * depth + soon + late + 3 * early + 4 * last
+    factors = sum(padded) * long * band * 12
+    limit = held * tile_bytes + panels.size * 4 + factors + 4 * 2**20
     any_spec = pl.BlockSpec(memory_space=pl.ANY)
-    return pl.pallas_call(
+    vmem_spec = pl.BlockSpec(memory_space=pltpu.VMEM)
+    merged, back = pl.pallas_call(
         functools.partial(whole_kernel, profile, group),
         in_specs=[pl.BlockSpec(memory_space=pltpu.SMEM), any_spec, any_spec],
-        out_specs=any_spec,
-        out_shape=jax.ShapeDtypeStruct(tiles.shape, tiles.dtype),
+        out_specs=[vmem_spec] * 2,
+        out_shape=[
+            jax.ShapeDtypeStruct(tiles.shape, f32),
+            jax.ShapeDtypeStruct((last, band, columns), f32),
+        ],
         scratch_shapes=scratch,
         compiler_params=pltpu.CompilerParams(
-            collective_id=1 + index, has_side_effects=True, vmem_limit_bytes=58 * 2**20
+            collective_id=1 + index, has_side_effects=True, vmem_limit_bytes=limit
         ),
     )(table, tiles, panels)
+    return settle(table, merged, back)
 
 
 def local(eigvec, reflectors, sweep_group):

time: 162 us -> 143 us (0.88); the launches traced: 160 us -> 143 us
  Pallas kernels: 154 us -> 142 us
  local copies, waits for them, and re-layouts: 4.66 us -> 0 us
    pallas_call x1, Pallas kernels: 144 us -> 129 us  [whole(): pl.pallas_call(functools.partial(whole_kernel, profile, group), in_specs=...]
    unnamed x1 -> x0, local copies, waits for them, and re-layouts: 4.66 us -> none
    pallas_call x0 -> x1, Pallas kernels: none -> 2.94 us  [settle(): pl.pallas_call(settle_kernel, in_specs=[pl.BlockSpec(memory_space=pltpu.S...]
where the time goes in v2:
time: 143 us
  Pallas kernels  142 us (99%)
    pallas_call x1, Pallas kernels, whole(): pl.pallas_call(functools.partial(whole_kernel, profile, group), in_specs=...  129 us
    pallas_call x1, Pallas kernels, plan(): pl.pallas_call(functools.partial(plan_kernel, profiles), out_shape=[jax.S...  9.91 us
    pallas_call x1, Pallas kernels, settle(): pl.pallas_call(settle_kernel, in_specs=[pl.BlockSpec(memory_space=pltpu.S...  2.94 us

profile of v2, /device:TPU:0, one launch (start us, length us, event | category | flops | bytes accessed | tf_op | source)
XLA Modules:
  0.0 143.0 jit_solution(6422411765133468533)
XLA Ops:
  0.0 9.9 %plan.1 = (s32[16,128]{1,0:T(8,128)S(1)}, s32[1]{0:T(128)}, s32[8,8,128]{2,1,0:T(8,128)S(1)}) custom-call(s32[2,32]{1,0:T(2,128)} %bitcast.51), custom_call_target="tpu_custom_call" | custom-call | tf_op jit(solution)/shard_map/plan/pallas_call | solution.py:476
  10.6 132.2 %conditional.1 = (f32[32,1,128,256]{3,2,1,0:T(8,128)}) conditional(s32[]{:T(128)} %bitcast.28, (s32[16,128]{1,0:T(8,128)S(1)}, f32[32,128,256]{2,1,0:T(8,128)}, f32[2,32,64,128]{3,2,1,0:T(8,128)}) %tuple.72, (s32[16,128]{1,0:T(8,128)S(1)}, f32[32,128,256]{2,1,0:T(8,128)}, f32[2,32,64,128]{3,2,1,0:T(8,128)}) %tuple.73, ...), branch_computations={%region_0.0_spmd, %region_1.0_spmd, %region_2.0_spmd, %region_3.0_... | conditional | flops 23761 | bytes 134228512 | solution.py:897
  10.9 128.7 %branch_4_fun.1 = (f32[32,128,256]{2,1,0:T(8,128)S(1)}, f32[15,128,256]{2,1,0:T(8,128)S(1)}) custom-call(s32[16,128]{1,0:T(8,128)S(1)} %get-tuple-element.85.table, f32[32,128,256]{2,1,0:T(8,128)} %get-tuple-element.86.tiles_in, f32[2,32,64,128]{3,2,1,0:T(8,128)} %get-tuple-element.87.panels_in), custom_call_target="tpu_custom_call" | custom-call | tf_op jit(solution)/shard_map/cond/branch_4_fun/pallas_call | solution.py:853
  139.6 2.9 %settle.11 = f32[32,128,256]{2,1,0:T(8,128)} custom-call(s32[16,128]{1,0:T(8,128)S(1)} %get-tuple-element.85.table, f32[32,128,256]{2,1,0:T(8,128)S(1)} %get-tuple-element.88.merged, f32[15,128,256]{2,1,0:T(8,128)S(1)} %get-tuple-element.89.back), custom_call_target="tpu_custom_call" | custom-call | tf_op jit(solution)/shard_map/cond/branch_4_fun/settle/pallas_call | solution.py:807
